TPU v7x, 32 devices: a whole 2x2x4 slice. The times are simulated.
32 devices in a mesh: row: 8 (over z, y), col: 4 (over x, core).
Axes of the slice: x: 2, y: 2, z: 4, core: 2. Of those that a mesh axis runs over, the one named last changes fastest.
Arguments:
- root_rhs: bfloat16 [8, 8192], replicated, may hold values from -6 to 6
- diag_inv: bfloat16 [16, 512, 512], replicated, may hold values from -1 to 2
- tile_u: bfloat16 [8, 4, 2, 4, 128, 512], P('row', 'col'), may hold values from -0.1875 to 0.1875
- tile_v: bfloat16 [8, 4, 2, 4, 512, 128], P('row', 'col'), may hold values from -0.25 to 0.25
- tile_rank: int32 [8, 4, 2, 4], P('row', 'col'), may hold values from 16 to 128
- child_x: bfloat16 [32, 8, 512], P(('row', 'col')), may hold values from -6 to 6
- border_t: bfloat16 [32, 512, 1024], P(('row', 'col')), may hold values from -0.09375 to 0.09375
- child_inv: bfloat16 [32, 512, 512], P(('row', 'col')), may hold values from -1 to 2
- child_blocks: int32 [32, 8], P(('row', 'col')), may hold values from 0 to 63
Outputs:
- root_solution: float32 [8, 8192], P(None, ('row', 'col'))
- child_out: float32 [32, 8, 512], P(('row', 'col'))
All inputs are finite; a program needn't handle non-finite values.
Results may differ from a plain program's by a relative error of at most 0.017.
Values sent between devices are 32-bit elements; how exact they have to be, the bound alone decides.
A program may use at most 64 MiB of HBM per device.

v0:
```python
import jax
import jax.numpy as jnp
from jax import lax
from jax.sharding import PartitionSpec as P

BLK = 128
BB = 8


def per_device(
    root_rhs, diag_inv, tile_u, tile_v, tile_rank, child_x, border_t, child_inv, child_blocks
):
    highest_precision = lax.Precision.HIGHEST
    n_row = lax.axis_size("row")
    n_col = lax.axis_size("col")
    my_row = lax.axis_index("row")
    my_col = lax.axis_index("col")
    ntile = diag_inv.shape[0]
    tile = diag_inv.shape[1]
    rhs_count = root_rhs.shape[0]
    rank_max = tile_u.shape[4]
    t_rows = tile_u.shape[2]
    t_cols = tile_u.shape[3]
    left_tiles = tile_u[0, 0]
    right_tiles = tile_v[0, 0]
    tile_ranks = tile_rank[0, 0]
    blocks_per_front = tile // BLK
    n_child = child_x.shape[0]
    upward = jnp.einsum("crs,csb->crb", child_x, border_t, preferred_element_type=jnp.float32)
    pieces = (
        upward.reshape(n_child, rhs_count, BB, BLK)
        .transpose(1, 0, 2, 3)
        .reshape(rhs_count, n_child * BB, BLK)
    )
    flat_blocks = child_blocks.reshape(-1)
    dense_sum = (
        jnp.zeros((rhs_count, ntile * blocks_per_front, BLK), jnp.float32)
        .at[:, flat_blocks, :]
        .add(pieces)
    )
    dense_sum = dense_sum.reshape(rhs_count, ntile, tile)
    right_side = root_rhs.reshape(rhs_count, ntile, tile)
    col_ids = my_col + n_col * jnp.arange(t_cols)
    row_ids = my_row + n_row * jnp.arange(t_rows)
    rank_iota = jnp.arange(rank_max)

    def forward(column, solved_rows):
        owner_slot = column // n_row
        on_row = column % n_row == my_row
        known_cols = jnp.take(solved_rows, col_ids, axis=1).astype(jnp.bfloat16)
        right_row = lax.dynamic_index_in_dim(right_tiles, owner_slot, 0, keepdims=False)
        left_row_index = lax.dynamic_index_in_dim(left_tiles, owner_slot, 0, keepdims=False)
        rank_row = lax.dynamic_index_in_dim(tile_ranks, owner_slot, 0, keepdims=False)
        live_mask = (rank_iota[None, :] < rank_row[:, None]) & (col_ids[:, None] < column) & on_row
        coefficient_values = jnp.einsum(
            "rbt,btq->rbq", known_cols, right_row, preferred_element_type=jnp.float32
        )
        coefficient_values = jnp.where(live_mask[None], coefficient_values, 0.0).astype(
            jnp.bfloat16
        )
        partial_value = jnp.einsum(
            "rbq,bqt->rt", coefficient_values, left_row_index, preferred_element_type=jnp.float32
        )
        carried = lax.dynamic_index_in_dim(dense_sum, column, 1, keepdims=False)
        row_total = lax.psum(partial_value + carried, ("row", "col"))
        block_rhs = lax.dynamic_index_in_dim(right_side, column, 1, keepdims=False).astype(
            jnp.float32
        )
        inverse = lax.dynamic_index_in_dim(diag_inv, column, 0, keepdims=False).astype(jnp.float32)
        fresh = jnp.dot(block_rhs - row_total, inverse, precision=highest_precision)
        return lax.dynamic_update_index_in_dim(solved_rows, fresh, column, 1)

    solved_rows = lax.fori_loop(0, ntile, forward, jnp.zeros((rhs_count, ntile, tile), jnp.float32))

    def backward(sweep, result):
        column = ntile - 1 - sweep
        owner_slot = column // n_col
        on_col = column % n_col == my_col
        known_rows = jnp.take(result, row_ids, axis=1).astype(jnp.bfloat16)
        left_col = lax.dynamic_index_in_dim(left_tiles, owner_slot, 1, keepdims=False)
        right_col = lax.dynamic_index_in_dim(right_tiles, owner_slot, 1, keepdims=False)
        rank_col = lax.dynamic_index_in_dim(tile_ranks, owner_slot, 1, keepdims=False)
        live_mask = (rank_iota[None, :] < rank_col[:, None]) & (row_ids[:, None] > column) & on_col
        coefficient_values = jnp.einsum(
            "rat,aqt->raq", known_rows, left_col, preferred_element_type=jnp.float32
        )
        coefficient_values = jnp.where(live_mask[None], coefficient_values, 0.0).astype(
            jnp.bfloat16
        )
        partial_value = jnp.einsum(
            "raq,atq->rt", coefficient_values, right_col, preferred_element_type=jnp.float32
        )
        col_total = lax.psum(partial_value, ("row", "col"))
        block_solved = lax.dynamic_index_in_dim(solved_rows, column, 1, keepdims=False)
        inverse = lax.dynamic_index_in_dim(diag_inv, column, 0, keepdims=False).astype(jnp.float32)
        fresh = jnp.dot(block_solved - col_total, inverse.T, precision=highest_precision)
        return lax.dynamic_update_index_in_dim(result, fresh, column, 1)

    result = lax.fori_loop(0, ntile, backward, jnp.zeros((rhs_count, ntile, tile), jnp.float32))
    share = ntile * tile // (n_row * n_col)
    start = (my_row * n_col + my_col) * share
    root_part = lax.dynamic_slice_in_dim(result.reshape(rhs_count, ntile * tile), start, share, 1)
    gathered = result.reshape(rhs_count, ntile * blocks_per_front, BLK)[:, flat_blocks, :]
    gathered = gathered.reshape(rhs_count, n_child, BB * BLK).astype(jnp.bfloat16)
    returned = jnp.einsum("rcb,csb->crs", gathered, border_t, preferred_element_type=jnp.float32)
    child_out = child_x.astype(jnp.float32) - jnp.einsum(
        "crs,cst->crt", returned, child_inv.astype(jnp.float32), precision=highest_precision
    )
    return (root_part, child_out)


def solution(mesh):
    return jax.shard_map(
        per_device,
        mesh=mesh,
        in_specs=(
            P(),
            P(),
            P("row", "col", None, None, None, None),
            P("row", "col", None, None, None, None),
            P("row", "col", None, None),
            P(("row", "col"), None, None),
            P(("row", "col"), None, None),
            P(("row", "col"), None, None),
            P(("row", "col"), None),
        ),
        out_specs=(P(None, ("row", "col")), P(("row", "col"), None, None)),
        check_vma=False,
    )
```

profile of v0, /device:TPU:0, one launch (start us, length us, event | category | flops | bytes accessed | tf_op | source)
XLA Modules:
  0.0 1424.5 jit_solution(4886888711580385367)
XLA Ops:
  5.8 715.3 %while.32 = (s32[]{:T(128)}, f32[8,16,512]{2,0,1:T(8,128)S(1)}, bf16[8,16,512]{2,1,0:T(8,128)(2,1)S(1)}, s32[2,4]{1,0:T(2,128)}, s32[]{:T(128)}, /*index=5*/bf16...) while((s32[]{:T(128)}, f32[8,16,512]{2,0,1:T(8,128)S(1)}, ...), condition=%wide.region_3.4_spmd.clone, body=%wide.region_1.3_spmd.clone.sunk | while | flops 33598024 | bytes 1818560 | solution.py:73
  9.0 42.0 %psum.32 = f32[8,512]{1,0:T(8,128)S(1)} all-reduce(f32[8,512]{1,0:T(8,128)S(1)} %fusion.106), channel_id=1, replica_groups=mesh['row'=8,'col'=4] {'row','col'}, use_global_device_ids=true, to_apply=%region_2.2 | all-reduce | flops 4096 | bytes 32768 | tf_op jit(solution)/shard_map/while/body/eval_jaxpr/psum | solution.py:65
  55.5 40.2 %psum.32 = f32[8,512]{1,0:T(8,128)S(1)} all-reduce(f32[8,512]{1,0:T(8,128)S(1)} %fusion.106), channel_id=1, replica_groups=mesh['row'=8,'col'=4] {'row','col'}, use_global_device_ids=true, to_apply=%region_2.2 | all-reduce | flops 4096 | bytes 32768 | tf_op jit(solution)/shard_map/while/body/eval_jaxpr/psum | solution.py:65
  100.2 39.9 %psum.32 = f32[8,512]{1,0:T(8,128)S(1)} all-reduce(f32[8,512]{1,0:T(8,128)S(1)} %fusion.106), channel_id=1, replica_groups=mesh['row'=8,'col'=4] {'row','col'}, use_global_device_ids=true, to_apply=%region_2.2 | all-reduce | flops 4096 | bytes 32768 | tf_op jit(solution)/shard_map/while/body/eval_jaxpr/psum | solution.py:65
  144.7 40.1 %psum.32 = f32[8,512]{1,0:T(8,128)S(1)} all-reduce(f32[8,512]{1,0:T(8,128)S(1)} %fusion.106), channel_id=1, replica_groups=mesh['row'=8,'col'=4] {'row','col'}, use_global_device_ids=true, to_apply=%region_2.2 | all-reduce | flops 4096 | bytes 32768 | tf_op jit(solution)/shard_map/while/body/eval_jaxpr/psum | solution.py:65
  189.3 39.9 %psum.32 = f32[8,512]{1,0:T(8,128)S(1)} all-reduce(f32[8,512]{1,0:T(8,128)S(1)} %fusion.106), channel_id=1, replica_groups=mesh['row'=8,'col'=4] {'row','col'}, use_global_device_ids=true, to_apply=%region_2.2 | all-reduce | flops 4096 | bytes 32768 | tf_op jit(solution)/shard_map/while/body/eval_jaxpr/psum | solution.py:65
  233.8 40.3 %psum.32 = f32[8,512]{1,0:T(8,128)S(1)} all-reduce(f32[8,512]{1,0:T(8,128)S(1)} %fusion.106), channel_id=1, replica_groups=mesh['row'=8,'col'=4] {'row','col'}, use_global_device_ids=true, to_apply=%region_2.2 | all-reduce | flops 4096 | bytes 32768 | tf_op jit(solution)/shard_map/while/body/eval_jaxpr/psum | solution.py:65
  278.5 39.8 %psum.32 = f32[8,512]{1,0:T(8,128)S(1)} all-reduce(f32[8,512]{1,0:T(8,128)S(1)} %fusion.106), channel_id=1, replica_groups=mesh['row'=8,'col'=4] {'row','col'}, use_global_device_ids=true, to_apply=%region_2.2 | all-reduce | flops 4096 | bytes 32768 | tf_op jit(solution)/shard_map/while/body/eval_jaxpr/psum | solution.py:65
  322.9 40.2 %psum.32 = f32[8,512]{1,0:T(8,128)S(1)} all-reduce(f32[8,512]{1,0:T(8,128)S(1)} %fusion.106), channel_id=1, replica_groups=mesh['row'=8,'col'=4] {'row','col'}, use_global_device_ids=true, to_apply=%region_2.2 | all-reduce | flops 4096 | bytes 32768 | tf_op jit(solution)/shard_map/while/body/eval_jaxpr/psum | solution.py:65
  367.6 39.8 %psum.32 = f32[8,512]{1,0:T(8,128)S(1)} all-reduce(f32[8,512]{1,0:T(8,128)S(1)} %fusion.106), channel_id=1, replica_groups=mesh['row'=8,'col'=4] {'row','col'}, use_global_device_ids=true, to_apply=%region_2.2 | all-reduce | flops 4096 | bytes 32768 | tf_op jit(solution)/shard_map/while/body/eval_jaxpr/psum | solution.py:65
  411.9 40.4 %psum.32 = f32[8,512]{1,0:T(8,128)S(1)} all-reduce(f32[8,512]{1,0:T(8,128)S(1)} %fusion.106), channel_id=1, replica_groups=mesh['row'=8,'col'=4] {'row','col'}, use_global_device_ids=true, to_apply=%region_2.2 | all-reduce | flops 4096 | bytes 32768 | tf_op jit(solution)/shard_map/while/body/eval_jaxpr/psum | solution.py:65
  456.8 39.7 %psum.32 = f32[8,512]{1,0:T(8,128)S(1)} all-reduce(f32[8,512]{1,0:T(8,128)S(1)} %fusion.106), channel_id=1, replica_groups=mesh['row'=8,'col'=4] {'row','col'}, use_global_device_ids=true, to_apply=%region_2.2 | all-reduce | flops 4096 | bytes 32768 | tf_op jit(solution)/shard_map/while/body/eval_jaxpr/psum | solution.py:65
  501.0 40.4 %psum.32 = f32[8,512]{1,0:T(8,128)S(1)} all-reduce(f32[8,512]{1,0:T(8,128)S(1)} %fusion.106), channel_id=1, replica_groups=mesh['row'=8,'col'=4] {'row','col'}, use_global_device_ids=true, to_apply=%region_2.2 | all-reduce | flops 4096 | bytes 32768 | tf_op jit(solution)/shard_map/while/body/eval_jaxpr/psum | solution.py:65
  590.0 40.5 %psum.32 = f32[8,512]{1,0:T(8,128)S(1)} all-reduce(f32[8,512]{1,0:T(8,128)S(1)} %fusion.106), channel_id=1, replica_groups=mesh['row'=8,'col'=4] {'row','col'}, use_global_device_ids=true, to_apply=%region_2.2 | all-reduce | flops 4096 | bytes 32768 | tf_op jit(solution)/shard_map/while/body/eval_jaxpr/psum | solution.py:65
  679.1 40.6 %psum.32 = f32[8,512]{1,0:T(8,128)S(1)} all-reduce(f32[8,512]{1,0:T(8,128)S(1)} %fusion.106), channel_id=1, replica_groups=mesh['row'=8,'col'=4] {'row','col'}, use_global_device_ids=true, to_apply=%region_2.2 | all-reduce | flops 4096 | bytes 32768 | tf_op jit(solution)/shard_map/while/body/eval_jaxpr/psum | solution.py:65
  721.9 700.1 %while.33 = (s32[]{:T(128)}, f32[8,16,512]{2,0,1:T(8,128)S(1)}, f32[8,16,512]{2,0,1:T(8,128)S(1)}, s32[2,4]{0,1:T(4,128)S(1)}, s32[]{:T(128)}, /*index=5*/bf16[2...) while((s32[]{:T(128)}, f32[8,16,512]{2,0,1:T(8,128)S(1)}, ...), condition=%wide.region_6.7_spmd.clone, body=%wide.region_4.6_spmd.clone.sunk | while | flops 29382456 | bytes 1203697 | solution.py:99
  767.2 40.7 %psum.33 = f32[8,512]{1,0:T(8,128)S(1)} all-reduce(f32[8,512]{1,0:T(8,128)S(1)} %fusion.113), channel_id=1, replica_groups=mesh['row'=8,'col'=4] {'row','col'}, use_global_device_ids=true, to_apply=%region_5.5 | all-reduce | flops 4096 | bytes 32768 | tf_op jit(solution)/shard_map/while/body/eval_jaxpr/psum | solution.py:93
  854.6 40.7 %psum.33 = f32[8,512]{1,0:T(8,128)S(1)} all-reduce(f32[8,512]{1,0:T(8,128)S(1)} %fusion.113), channel_id=1, replica_groups=mesh['row'=8,'col'=4] {'row','col'}, use_global_device_ids=true, to_apply=%region_5.5 | all-reduce | flops 4096 | bytes 32768 | tf_op jit(solution)/shard_map/while/body/eval_jaxpr/psum | solution.py:93
  942.1 40.8 %psum.33 = f32[8,512]{1,0:T(8,128)S(1)} all-reduce(f32[8,512]{1,0:T(8,128)S(1)} %fusion.113), channel_id=1, replica_groups=mesh['row'=8,'col'=4] {'row','col'}, use_global_device_ids=true, to_apply=%region_5.5 | all-reduce | flops 4096 | bytes 32768 | tf_op jit(solution)/shard_map/while/body/eval_jaxpr/psum | solution.py:93
  1029.6 40.8 %psum.33 = f32[8,512]{1,0:T(8,128)S(1)} all-reduce(f32[8,512]{1,0:T(8,128)S(1)} %fusion.113), channel_id=1, replica_groups=mesh['row'=8,'col'=4] {'row','col'}, use_global_device_ids=true, to_apply=%region_5.5 | all-reduce | flops 4096 | bytes 32768 | tf_op jit(solution)/shard_map/while/body/eval_jaxpr/psum | solution.py:93
  1117.1 40.8 %psum.33 = f32[8,512]{1,0:T(8,128)S(1)} all-reduce(f32[8,512]{1,0:T(8,128)S(1)} %fusion.113), channel_id=1, replica_groups=mesh['row'=8,'col'=4] {'row','col'}, use_global_device_ids=true, to_apply=%region_5.5 | all-reduce | flops 4096 | bytes 32768 | tf_op jit(solution)/shard_map/while/body/eval_jaxpr/psum | solution.py:93
  1204.6 40.8 %psum.33 = f32[8,512]{1,0:T(8,128)S(1)} all-reduce(f32[8,512]{1,0:T(8,128)S(1)} %fusion.113), channel_id=1, replica_groups=mesh['row'=8,'col'=4] {'row','col'}, use_global_device_ids=true, to_apply=%region_5.5 | all-reduce | flops 4096 | bytes 32768 | tf_op jit(solution)/shard_map/while/body/eval_jaxpr/psum | solution.py:93
  1292.1 40.8 %psum.33 = f32[8,512]{1,0:T(8,128)S(1)} all-reduce(f32[8,512]{1,0:T(8,128)S(1)} %fusion.113), channel_id=1, replica_groups=mesh['row'=8,'col'=4] {'row','col'}, use_global_device_ids=true, to_apply=%region_5.5 | all-reduce | flops 4096 | bytes 32768 | tf_op jit(solution)/shard_map/while/body/eval_jaxpr/psum | solution.py:93
  1379.7 40.8 %psum.33 = f32[8,512]{1,0:T(8,128)S(1)} all-reduce(f32[8,512]{1,0:T(8,128)S(1)} %fusion.113), channel_id=1, replica_groups=mesh['row'=8,'col'=4] {'row','col'}, use_global_device_ids=true, to_apply=%region_5.5 | all-reduce | flops 4096 | bytes 32768 | tf_op jit(solution)/shard_map/while/body/eval_jaxpr/psum | solution.py:93
  (286 shorter events, 532.4 us)
Async XLA Ops:
  0.6 1422.9 %copy-start = (bf16[1,512,512]{2,1,0:T(8,128)(2,1)S(1)}, bf16[1,512,512]{2,1,0:T(8,128)(2,1)}, u32[]{:S(2)}) copy-start(bf16[1,512,512]{2,1,0:T(8,128)(2,1)} %param.20) | copy-start | bytes 1572868
  5.7 1417.4 %copy-start.1 = (bf16[1,512,1024]{2,1,0:T(8,128)(2,1)S(1)}, bf16[1,512,1024]{2,1,0:T(8,128)(2,1)}, u32[]{:S(2)}) copy-start(bf16[1,512,1024]{2,1,0:T(8,128)(2,1)} %param.19) | copy-start | bytes 3145732
  5.8 1417.8 %copy-start.2 = (bf16[1,8,512]{2,1,0:T(8,128)(2,1)S(1)}, bf16[1,8,512]{2,1,0:T(8,128)(2,1)}, u32[]{:S(2)}) copy-start(bf16[1,8,512]{2,1,0:T(8,128)(2,1)} %param.18) | copy-start | bytes 24580
where the time goes:
time: 1430 us; the launch traced here: 1420 us
  blocking collectives  1280 us (90%)
  matrix products  100 us (7%)
  local copies, waits for them, and re-layouts  33.4 us (2%)
    psum x16, blocking collectives, forward(): row_total = lax.psum(partial_value + carried, ('row', 'col'))  643 us
    psum x16, blocking collectives, backward(): col_total = lax.psum(partial_value, ('row', 'col'))  641 us

commit v1 on v0

v1 whole, which is shorter than its diff:
```python
import functools
import jax
import jax.numpy as jnp
from jax import lax
from jax.experimental import pallas as pl
from jax.experimental.pallas import tpu as pltpu
from jax.sharding import PartitionSpec as P

BLK = 128
F32 = jnp.float32
BF16 = jnp.bfloat16
MESH = pl.DeviceIdType.MESH
NN = (((1,), (0,)), ((), ()))
NT = (((1,), (1,)), ((), ()))


def dot(a, b, dims=NN):
    return lax.dot_general(a, b, dims, preferred_element_type=F32)


def two_part(a):
    high = a.astype(BF16).astype(F32)
    return jnp.concatenate([high, a - high], axis=0).astype(BF16)


def wide_dot(a, b, dims=NN):
    n = a.shape[0]
    both = dot(two_part(a), b, dims)
    return both[:n] + both[n:]


def solve_kernel(
    n_row, n_col, t_rows, t_cols, ntile, n_child, bb, share,
    rhs_hbm, dinv_hbm, u_hbm, v_hbm, rank_ref, cx_ref, bt_hbm, ci_hbm, cb_ref,
    root_out, child_out,
    rhs, drow, dcol, u, v, bt, ci, w, y,
    csum, csum_in, acc, fpart, xs, bacc, bpart, z_all,
    load_sem, csend, crecv, fsend, frecv, bsend, brecv, zsend, zrecv,
):
    r = lax.axis_index("row")
    c = lax.axis_index("col")
    n_dev = n_row * n_col
    me = r * n_col + c
    rhs_count, tile = acc.shape[1], acc.shape[2]
    rank_max = u.shape[2]
    per = tile // BLK
    i_max = r + n_row * (t_rows - 1)

    barrier = pltpu.get_barrier_semaphore()

    def greet(o, carry):
        other = lax.rem(me + o, n_dev)
        pl.semaphore_signal(
            barrier, inc=1, device_id=(other // n_col, lax.rem(other, n_col)), device_id_type=MESH
        )
        return carry

    lax.fori_loop(1, n_dev, greet, 0)

    loads = []

    def load(src, dst):
        copy = pltpu.make_async_copy(src, dst, load_sem.at[len(loads)])
        loads.append(copy)
        copy.start()
        return copy

    bt_load = load(bt_hbm, bt)
    row_loads = [load(dinv_hbm.at[r + n_row * a], drow.at[a]) for a in range(t_rows)]
    row_loads += [
        load(rhs_hbm.at[:, pl.ds(pl.multiple_of((r + n_row * a) * tile, tile), tile)], rhs.at[a])
        for a in range(t_rows)
    ]
    u_load = load(u_hbm, u)
    v_load = load(v_hbm, v)
    col_loads = [load(dinv_hbm.at[c + n_col * b], dcol.at[b]) for b in range(t_cols)]
    ci_load = load(ci_hbm, ci)

    for b in range(t_cols):
        bacc[b] = jnp.zeros((rhs_count, tile), F32)

    def need(row, k):
        return (row + n_row * (t_rows - 1) > k) | (row == lax.rem(k, n_row))

    for a in range(t_rows):
        for rr in range(n_row):
            @pl.when(jnp.logical_not(need(rr, r + n_row * a)))
            def _():
                bpart[a, rr] = jnp.zeros((rhs_count, tile), F32)

    bt_load.wait()
    ups = []
    for ch in range(n_child):
        up = dot(cx_ref[ch], bt[ch])
        ups.append([up[:, m * BLK:(m + 1) * BLK] for m in range(bb)])

    def spread(j, carry):
        row = lax.rem(j, n_row)
        slot = j // n_row
        for q in range(per):
            total = jnp.zeros((rhs_count, BLK), F32)
            for ch in range(n_child):
                for m in range(bb):
                    hit = jnp.where(cb_ref[ch, m] == j * per + q, 1.0, 0.0).astype(F32)
                    total = total + ups[ch][m] * hit
            csum[row, slot, :, q * BLK:(q + 1) * BLK] = total
        return carry

    lax.fori_loop(0, ntile, spread, 0)
    pl.semaphore_wait(barrier, n_dev - 1)

    def csum_copy(rr, slot):
        return pltpu.make_async_remote_copy(
            src_ref=csum.at[rr], dst_ref=csum_in.at[slot],
            send_sem=csend.at[rr], recv_sem=crecv.at[slot],
            device_id=(rr, c), device_id_type=MESH,
        )

    def csum_start(o, carry):
        csum_copy(lax.rem(r + o, n_row), r).start()
        return carry

    lax.fori_loop(1, n_row, csum_start, 0)

    for copy in row_loads:
        copy.wait()
    u_load.wait()

    def fold_left(t, carry):
        a = t // t_cols
        b = lax.rem(t, t_cols)
        full = dot(u[a, b], drow[a])
        high = full.astype(BF16)
        w[a, b, :rank_max] = high
        w[a, b, rank_max:] = (full - high.astype(F32)).astype(BF16)
        return carry

    lax.fori_loop(0, t_rows * t_cols, fold_left, 0)

    def csum_wait(o, carry):
        rr = lax.rem(r + o, n_row)
        csum_copy(rr, rr).wait_recv()
        return carry

    lax.fori_loop(1, n_row, csum_wait, 0)
    for a in range(t_rows):
        base = -csum[r, a]
        for o in range(1, n_row):
            base = base - csum_in[lax.rem(r + o, n_row), a]
        base = base + rhs[a].astype(F32) * jnp.where(c == 0, 1.0, 0.0).astype(F32)
        acc[a] = wide_dot(base, drow[a])

    def row_copy(a, rr, slot_b, slot_c, target_col):
        return pltpu.make_async_remote_copy(
            src_ref=acc.at[a], dst_ref=fpart.at[slot_b, slot_c],
            send_sem=fsend.at[a, rr], recv_sem=frecv.at[slot_b, slot_c],
            device_id=(rr, target_col), device_id_type=MESH,
        )

    def each_row_copy(a, act, own):
        i = r + n_row * a
        slot_b = i // n_col
        target = lax.rem(i, n_col)

        def one(t, carry):
            rr = lax.rem(r + t, n_row)

            @pl.when(need(rr, i))
            def _():
                act(row_copy(a, rr, slot_b, c, target))

            return carry

        lax.fori_loop(1, n_row, one, 0)

        @pl.when(target != c)
        def _():
            act(row_copy(a, r, slot_b, c, target))

        if own:
            @pl.when(target == c)
            def _():
                fpart[slot_b, c] = acc[a]

    def send_row(a):
        each_row_copy(a, lambda copy: copy.start(), True)

    def col_copy(b, cc, slot_a, slot_r, target_row):
        return pltpu.make_async_remote_copy(
            src_ref=bacc.at[b], dst_ref=bpart.at[slot_a, slot_r],
            send_sem=bsend.at[b, cc], recv_sem=brecv.at[slot_a, slot_r],
            device_id=(target_row, cc), device_id_type=MESH,
        )

    def each_col_copy(b, act, own):
        j = c + n_col * b
        slot_a = j // n_row
        target = lax.rem(j, n_row)
        for t in range(1, n_col):
            act(col_copy(b, lax.rem(c + n_col - t, n_col), slot_a, r, target))

        @pl.when(target != r)
        def _():
            act(col_copy(b, c, slot_a, r, target))

        if own:
            @pl.when(target == r)
            def _():
                bpart[slot_a, r] = bacc[b]

    def send_col(b):
        each_col_copy(b, lambda copy: copy.start(), True)

    lanes = lax.broadcasted_iota(jnp.int32, (rhs_count, rank_max), 1)

    def live(value, a, b):
        kept = jnp.where(lanes < rank_ref[a, b], value, 0.0).astype(BF16)
        return jnp.concatenate([kept, kept], axis=1)

    for a in range(t_rows):
        @pl.when(r + n_row * a <= c)
        def _():
            send_row(a)

    v_load.wait()
    for copy in col_loads:
        copy.wait()

    def forward(b, carry):
        k = c + n_col * b
        k_row = lax.rem(k, n_row)

        @pl.when(need(r, k))
        def _():
            for cc in range(n_col):
                @pl.when(jnp.logical_not((r == k_row) & (c == cc)))
                def _():
                    row_copy(0, lax.rem(r + 1, n_row), b, cc, c).wait_recv()

            x = fpart[b, 0]
            for cc in range(1, n_col):
                x = x + fpart[b, cc]
            xs[b] = x
            xb = x.astype(BF16)
            for a in range(t_rows):
                i = r + n_row * a

                @pl.when(i > k)
                def _():
                    p = live(dot(xb, v[a, b]), a, b)
                    acc[a] = acc[a] - dot(p, w[a, b])

                    @pl.when(i <= k + n_col)
                    def _():
                        send_row(a)

            @pl.when(r == k_row)
            def _():
                bacc[b] = wide_dot(xs[b], drow[k // n_row], NT)

                @pl.when(k >= i_max)
                def _():
                    send_col(b)

        @pl.when(b == 0)
        def _():
            def fold_right(t, inner):
                a = t // t_cols
                bq = lax.rem(t, t_cols)
                full = dot(dcol[bq], v[a, bq])
                high = full.astype(BF16)
                y[a, bq, :, :rank_max] = high
                y[a, bq, :, rank_max:] = (full - high.astype(F32)).astype(BF16)
                return inner

            lax.fori_loop(0, t_rows * t_cols, fold_right, 0)

        return carry

    lax.fori_loop(0, t_cols, forward, 0)

    def z_copy(a, rr, i):
        part = z_all.at[pl.ds(i * per, per)]
        return pltpu.make_async_remote_copy(
            src_ref=part, dst_ref=part, send_sem=zsend.at[a, rr], recv_sem=zrecv.at[i],
            device_id=(rr, c), device_id_type=MESH,
        )

    for a in reversed(range(t_rows)):
        i = r + n_row * a
        i_col = lax.rem(i, n_col)

        def wait_part(rr, carry):
            @pl.when(need(rr, i) & jnp.logical_not((rr == r) & (c == i_col)))
            def _():
                col_copy(0, lax.rem(c + 1, n_col), a, rr, r).wait_recv()

            return carry

        lax.fori_loop(0, n_row, wait_part, 0)
        z = bpart[a, 0]
        for rr in range(1, n_row):
            z = z + bpart[a, rr]
        for q in range(per):
            z_all[i * per + q] = z[:, q * BLK:(q + 1) * BLK]
        zb = z.astype(BF16)

        def back(t, carry):
            b = t_cols - 1 - t
            j = c + n_col * b

            @pl.when(j < i)
            def _():
                q = live(dot(zb, u[a, b], NT), a, b)
                bacc[b] = bacc[b] - dot(q, y[a, b], NT)

                @pl.when(j >= i - n_row)
                def _():
                    send_col(b)

            return carry

        lax.fori_loop(0, t_cols, back, 0)

        def z_start(o, carry):
            z_copy(a, lax.rem(r + o, n_row), i).start()
            return carry

        lax.fori_loop(1, n_row, z_start, 0)

    def z_wait(j, carry):
        @pl.when(lax.rem(j, n_row) != r)
        def _():
            z_copy(0, lax.rem(r + 1, n_row), j).wait_recv()

        return carry

    lax.fori_loop(0, ntile, z_wait, 0)

    if share % BLK == 0:
        for q in range(share // BLK):
            root_out[:, q * BLK:(q + 1) * BLK] = z_all[me * (share // BLK) + q]
    else:
        first = (me * share) // BLK
        root_out[...] = z_all[first]
    ci_load.wait()
    for ch in range(n_child):
        taken = jnp.concatenate([z_all[cb_ref[ch, m]] for m in range(bb)], axis=1).astype(BF16)
        returned = dot(taken, bt[ch], NT)
        child_out[ch] = cx_ref[ch].astype(F32) - wide_dot(returned, ci[ch])

    def csum_done(o, carry):
        csum_copy(lax.rem(r + o, n_row), r).wait_send()
        return carry

    lax.fori_loop(1, n_row, csum_done, 0)
    for a in range(t_rows):
        each_row_copy(a, lambda copy: copy.wait_send(), False)

        def z_done(o, carry):
            z_copy(a, lax.rem(r + o, n_row), r + n_row * a).wait_send()
            return carry

        lax.fori_loop(1, n_row, z_done, 0)
    for b in range(t_cols):
        @pl.when(need(r, c + n_col * b))
        def _():
            each_col_copy(b, lambda copy: copy.wait_send(), False)


def per_device(
    root_rhs, diag_inv, tile_u, tile_v, tile_rank, child_x, border_t, child_inv, child_blocks
):
    n_row = lax.axis_size("row")
    n_col = lax.axis_size("col")
    ntile, tile = diag_inv.shape[0], diag_inv.shape[1]
    rhs_count = root_rhs.shape[0]
    t_rows, t_cols, rank_max = tile_u.shape[2], tile_u.shape[3], tile_u.shape[4]
    n_child, bb = child_blocks.shape
    share = ntile * tile // (n_row * n_col)
    width = share if share % BLK == 0 else BLK
    vec = (rhs_count, tile)
    any_spec = pl.BlockSpec(memory_space=pl.ANY)
    vmem = pl.BlockSpec(memory_space=pltpu.VMEM)
    smem = pl.BlockSpec(memory_space=pltpu.SMEM)
    dma = pltpu.SemaphoreType.DMA
    root, child = pl.pallas_call(
        functools.partial(
            solve_kernel, n_row, n_col, t_rows, t_cols, ntile, n_child, bb, share
        ),
        out_shape=(
            jax.ShapeDtypeStruct((rhs_count, width), F32),
            jax.ShapeDtypeStruct(child_x.shape, F32),
        ),
        in_specs=[any_spec, any_spec, any_spec, any_spec, smem, vmem, any_spec, any_spec, smem],
        out_specs=(vmem, vmem),
        scratch_shapes=[
            pltpu.VMEM((t_rows,) + vec, BF16),
            pltpu.VMEM((t_rows, tile, tile), BF16),
            pltpu.VMEM((t_cols, tile, tile), BF16),
            pltpu.VMEM(tile_u.shape[2:], BF16),
            pltpu.VMEM(tile_v.shape[2:], BF16),
            pltpu.VMEM(border_t.shape, BF16),
            pltpu.VMEM(child_inv.shape, BF16),
            pltpu.VMEM((t_rows, t_cols, 2 * rank_max, tile), BF16),
            pltpu.VMEM((t_rows, t_cols, tile, 2 * rank_max), BF16),
            pltpu.VMEM((n_row, t_rows) + vec, F32),
            pltpu.VMEM((n_row, t_rows) + vec, F32),
            pltpu.VMEM((t_rows,) + vec, F32),
            pltpu.VMEM((t_cols, n_col) + vec, F32),
            pltpu.VMEM((t_cols,) + vec, F32),
            pltpu.VMEM((t_cols,) + vec, F32),
            pltpu.VMEM((t_rows, n_row) + vec, F32),
            pltpu.VMEM((ntile * tile // BLK, rhs_count, BLK), F32),
            dma((4 + 2 * t_rows + t_cols,)),
            dma((n_row,)),
            dma((n_row,)),
            dma((t_rows, n_row)),
            dma((t_cols, n_col)),
            dma((t_cols, n_col)),
            dma((t_rows, n_row)),
            dma((t_rows, n_row)),
            dma((ntile,)),
        ],
        compiler_params=pltpu.CompilerParams(collective_id=0, has_side_effects=True),
    )(
        root_rhs, diag_inv, tile_u[0, 0], tile_v[0, 0], tile_rank[0, 0],
        child_x, border_t, child_inv, child_blocks,
    )
    if width != share:
        me = lax.axis_index("row") * n_col + lax.axis_index("col")
        root = lax.dynamic_slice_in_dim(root, (me * share) % BLK, share, 1)
    return root, child


def solution(mesh):
    return jax.shard_map(
        per_device,
        mesh=mesh,
        in_specs=(
            P(),
            P(),
            P("row", "col", None, None, None, None),
            P("row", "col", None, None, None, None),
            P("row", "col", None, None),
            P(("row", "col"), None, None),
            P(("row", "col"), None, None),
            P(("row", "col"), None, None),
            P(("row", "col"), None),
        ),
        out_specs=(P(None, ("row", "col")), P(("row", "col"), None, None)),
        check_vma=False,
    )
```

time: 1430 us -> 117 us (0.08)
  blocking collectives: 1280 us -> 0 us
  Pallas kernels: 0 us -> 114 us
  matrix products: 100 us -> 0 us
  local copies, waits for them, and re-layouts: 33.4 us -> 2.62 us
    psum x32 -> x0, blocking collectives: 1280 us -> none  [the longest x16 643 us: forward(): row_total = lax.psum(partial_value + carried, ('row', 'col'))]
    pallas_call x0 -> x1, Pallas kernels: none -> 114 us  [per_device(): pl.pallas_call(functools.partial(solve_kernel, n_row, n_col, t_rows, t_co...]
    dot_general x67 -> x0, matrix products: 100 us -> none  [the longest x16 28.5 us: forward(): jnp.einsum('rbq,bqt->rt', coefficient_values, left_row_index, preferred_e...]
    gather x33 -> x0, local copies, waits for them, and re-layouts: 18.2 us -> none  [the longest x16 8.82 us: forward(): known_cols = jnp.take(solved_rows, col_ids, axis=1).astype(jnp.bfloat16)]
where the time goes in v1:
time: 117 us
  Pallas kernels  114 us (97%)
  local copies, waits for them, and re-layouts  2.62 us (2%)
    pallas_call x1, Pallas kernels, per_device(): pl.pallas_call(functools.partial(solve_kernel, n_row, n_col, t_rows, t_co...  114 us
    unnamed x2, local copies, waits for them, and re-layouts  2.62 us

profile of v1, /device:TPU:0, one launch (start us, length us, event | category | flops | bytes accessed | tf_op | source)
XLA Modules:
  0.0 117.1 jit_solution(5554888650696890787)
XLA Ops:
  0.6 113.8 %shard_map.104 = (f32[8,256]{1,0:T(8,128)}, f32[1,8,512]{2,1,0:T(8,128)}) custom-call(bf16[8,8192]{1,0:T(8,128)(2,1)} %rhs_hbm.1, bf16[16,512,512]{2,1,0:T(8,128)(2,1)} %dinv_hbm.1, bf16[2,4,128,512]{3,2,1,0:T(8,128)(2,1)} %bitcast.3, bf16[2,4,512,128]{3,2,1,0:T(8,128)(2,1)} %bitcast.4, s32[2,4]{1,0:T(2,128)} %bitcast.5, bf16[1,8,512]{2,1,0:T(8,128)(2,1)} %cx_ref.1, ...), custom_call_target="tpu_custom_call" | custom-call | tf_op jit(solution)/shard_map/pallas_call | solution.py:387
  114.4 1.3 %copy.13 = f32[8,256]{1,0:T(8,128)} copy(f32[8,256]{1,0:T(8,128)} %get-tuple-element.4) | data formatting | bytes 16384
  115.7 1.3 %copy.14 = f32[1,8,512]{2,1,0:T(8,128)} copy(f32[1,8,512]{2,1,0:T(8,128)} %get-tuple-element.5) | data formatting | bytes 32768

commit v2 on v1

--- a/solution.py
+++ b/solution.py
@@ -34,8 +34,10 @@
     rhs_hbm, dinv_hbm, u_hbm, v_hbm, rank_ref, cx_ref, bt_hbm, ci_hbm, cb_ref,
     root_out, child_out,
     rhs, drow, dcol, u, v, bt, ci, w, y,
-    csum, csum_in, acc, fpart, xs, bacc, bpart, z_all,
-    load_sem, csend, crecv, fsend, frecv, bsend, brecv, zsend, zrecv,
+    csum, csum_in, acc, fpart, epart, xs, bacc, bpart, opart, z_all,
+    out_v, out_w, out_u, out_y, in_v, in_w, in_u, in_y, pair_v, pair_w, pair_u, pair_y,
+    load_sem, csend, crecv, fsend, frecv, gsend, erecv, bsend, brecv, hsend, orecv,
+    xsend, xrecv, zsend, zrecv, esend, tsend, trecv, ssend, srecv,
 ):
     r = lax.axis_index("row")
     c = lax.axis_index("col")
@@ -82,11 +84,44 @@
     def need(row, k):
         return (row + n_row * (t_rows - 1) > k) | (row == lax.rem(k, n_row))
 
+    r_odd = lax.rem(r, 2) == 1
+    c_odd = lax.rem(c, 2) == 1
+
+    def below(i):
+        return i - lax.rem(i, 2)
+
+    def above(j):
+        return j + 1 - lax.rem(j, 2)
+
+    def need_back(row, j):
+        return (row + n_row * (t_rows - 1) > above(j)) | (row == lax.rem(j, n_row))
+
+    def fast_rows(odd):
+        last = odd == ntile - 1
+        first = jnp.where(last, lax.rem(odd, n_row), lax.rem(odd + 1, n_row))
+        return first, lax.rem(odd + 2, n_row), jnp.logical_not(last)
+
+    def is_fast_row(row, odd):
+        first, second, both = fast_rows(odd)
+        return (row == first) | (both & (row == second))
+
+    def fast_cols(even):
+        return lax.rem(even + n_col - 1, n_col), lax.rem(even + n_col - 2, n_col)
+
+    def is_fast_col(col, even):
+        first, second = fast_cols(even)
+        return (col == first) | (col == second)
+
     for a in range(t_rows):
+        i = r + n_row * a
         for rr in range(n_row):
-            @pl.when(jnp.logical_not(need(rr, r + n_row * a)))
+            @pl.when(jnp.logical_not(need_back(rr, i)))
             def _():
                 bpart[a, rr] = jnp.zeros((rhs_count, tile), F32)
+
+            @pl.when(jnp.logical_not(need_back(rr, i + 1)))
+            def _():
+                opart[a, rr] = jnp.zeros((rhs_count, tile), F32)
 
     bt_load.wait()
     ups = []
@@ -136,6 +171,65 @@
         return carry
 
     lax.fori_loop(0, t_rows * t_cols, fold_left, 0)
+    v_load.wait()
+
+    def owns(a):
+        return r_odd & (lax.rem(r + n_row * a + n_col - 1, n_col) == c)
+
+    def pair_copy(src, dst, send, recv, device):
+        return pltpu.make_async_remote_copy(
+            src_ref=src, dst_ref=dst, send_sem=send, recv_sem=recv,
+            device_id=device, device_id_type=MESH,
+        )
+
+    def each_forward_pair(a, act):
+        odd = r + n_row * a
+        slot = odd // n_col
+        col = lax.rem(odd, n_col)
+        first, second, both = fast_rows(odd)
+
+        def to(row, t):
+            act(pair_copy(out_v.at[a], in_v.at[slot], tsend.at[a, t, 0], trecv.at[slot, 0], (row, col)))
+            act(pair_copy(out_w.at[a], in_w.at[slot], tsend.at[a, t, 1], trecv.at[slot, 1], (row, col)))
+
+        to(first, 0)
+
+        @pl.when(both)
+        def _():
+            to(second, 1)
+
+    def each_backward_pair(a, act):
+        even = r + n_row * a - 1
+        slot = even // n_row
+        row = lax.rem(even, n_row)
+        for t, col in enumerate(fast_cols(even)):
+            act(pair_copy(out_u.at[a], in_u.at[slot], ssend.at[a, t, 0], srecv.at[slot, 0], (row, col)))
+            act(pair_copy(out_y.at[a], in_y.at[slot], ssend.at[a, t, 1], srecv.at[slot, 1], (row, col)))
+
+    def start(copy):
+        copy.start()
+
+    def send_forward_pair(a):
+        @pl.when(owns(a))
+        def _():
+            b = (r + n_row * a - 1) // n_col
+            rank = rank_ref[a, b]
+            keep = lax.broadcasted_iota(jnp.int32, (tile, rank_max), 1) < rank
+            out_v[a] = jnp.where(keep, v[a, b].astype(F32), 0.0)
+            out_w[a] = w[a, b, :rank_max].astype(F32) + w[a, b, rank_max:].astype(F32)
+            each_forward_pair(a, start)
+
+    def send_backward_pair(a):
+        @pl.when(owns(a))
+        def _():
+            b = (r + n_row * a - 1) // n_col
+            rank = rank_ref[a, b]
+            keep = lax.broadcasted_iota(jnp.int32, (rank_max, tile), 0) < rank
+            out_u[a] = jnp.where(keep, u[a, b].astype(F32), 0.0)
+            out_y[a] = y[a, b, :, :rank_max].astype(F32) + y[a, b, :, rank_max:].astype(F32)
+            each_backward_pair(a, start)
+
+    send_forward_pair(0)
 
     def csum_wait(o, carry):
         rr = lax.rem(r + o, n_row)
@@ -157,33 +251,92 @@
             device_id=(rr, target_col), device_id_type=MESH,
         )
 
+    def fast_row_copy(a, t, rr, slot_b, slot_c, target_col, odd):
+        dst, sem = (fpart, frecv) if odd else (epart, erecv)
+        return pltpu.make_async_remote_copy(
+            src_ref=acc.at[a], dst_ref=dst.at[slot_b, slot_c],
+            send_sem=gsend.at[a, t], recv_sem=sem.at[slot_b, slot_c],
+            device_id=(rr, target_col), device_id_type=MESH,
+        )
+
     def each_row_copy(a, act, own):
         i = r + n_row * a
+        odd = above(i)
+        odd_slot = odd // n_col
+        odd_col = lax.rem(odd, n_col)
+        first, second, both = fast_rows(odd)
         slot_b = i // n_col
         target = lax.rem(i, n_col)
 
-        def one(t, carry):
-            rr = lax.rem(r + t, n_row)
-
-            @pl.when(need(rr, i))
-            def _():
-                act(row_copy(a, rr, slot_b, c, target))
-
-            return carry
-
-        lax.fori_loop(1, n_row, one, 0)
-
-        @pl.when(target != c)
-        def _():
-            act(row_copy(a, r, slot_b, c, target))
-
-        if own:
-            @pl.when(target == c)
-            def _():
-                fpart[slot_b, c] = acc[a]
+        @pl.when(r_odd)
+        def _():
+            here = (first == r) & (odd_col == c)
+
+            @pl.when(jnp.logical_not(here))
+            def _():
+                act(fast_row_copy(a, 0, first, odd_slot, c, odd_col, True))
+
+            if own:
+                @pl.when(here)
+                def _():
+                    fpart[odd_slot, c] = acc[a]
+
+            @pl.when(both)
+            def _():
+                act(fast_row_copy(a, 1, second, odd_slot, c, odd_col, True))
+
+        @pl.when(jnp.logical_not(r_odd))
+        def _():
+            act(fast_row_copy(a, 0, first, odd_slot, c, odd_col, False))
+
+            @pl.when(both)
+            def _():
+                act(fast_row_copy(a, 1, second, odd_slot, c, odd_col, False))
+
+            def one(t, carry):
+                rr = lax.rem(r + t, n_row)
+
+                @pl.when(need(rr, i))
+                def _():
+                    act(row_copy(a, rr, slot_b, c, target))
+
+                return carry
+
+            lax.fori_loop(1, n_row, one, 0)
+
+            @pl.when(target != c)
+            def _():
+                act(row_copy(a, r, slot_b, c, target))
+
+            if own:
+                @pl.when(target == c)
+                def _():
+                    fpart[slot_b, c] = acc[a]
 
     def send_row(a):
-        each_row_copy(a, lambda copy: copy.start(), True)
+        each_row_copy(a, start, True)
+
+    def x_copy(b, rr):
+        return pltpu.make_async_remote_copy(
+            src_ref=xs.at[b], dst_ref=xs.at[b], send_sem=xsend.at[b, rr], recv_sem=xrecv.at[b],
+            device_id=(rr, c), device_id_type=MESH,
+        )
+
+    def each_x_copy(b, act):
+        k = c + n_col * b
+
+        @pl.when(c_odd & (k < ntile - 1) & (r == lax.rem(k + 1, n_row)))
+        def _():
+            def one(t, carry):
+                rr = lax.rem(r + t, n_row)
+
+                @pl.when(need(rr, k) & jnp.logical_not(is_fast_row(rr, k)))
+                def _():
+                    act(x_copy(b, rr))
+
+                return carry
+
+            lax.fori_loop(1, n_row, one, 0)
 
     def col_copy(b, cc, slot_a, slot_r, target_row):
         return pltpu.make_async_remote_copy(
@@ -192,24 +345,45 @@
             device_id=(target_row, cc), device_id_type=MESH,
         )
 
+    def fast_col_copy(b, t, cc, slot_a, slot_r, target_row, odd):
+        dst, sem = (opart, orecv) if odd else (bpart, brecv)
+        return pltpu.make_async_remote_copy(
+            src_ref=bacc.at[b], dst_ref=dst.at[slot_a, slot_r],
+            send_sem=hsend.at[b, t], recv_sem=sem.at[slot_a, slot_r],
+            device_id=(target_row, cc), device_id_type=MESH,
+        )
+
     def each_col_copy(b, act, own):
         j = c + n_col * b
+        even = below(j)
+        even_slot = even // n_row
+        even_row = lax.rem(even, n_row)
         slot_a = j // n_row
         target = lax.rem(j, n_row)
-        for t in range(1, n_col):
-            act(col_copy(b, lax.rem(c + n_col - t, n_col), slot_a, r, target))
-
-        @pl.when(target != r)
-        def _():
-            act(col_copy(b, c, slot_a, r, target))
-
-        if own:
-            @pl.when(target == r)
-            def _():
-                bpart[slot_a, r] = bacc[b]
+
+        @pl.when(jnp.logical_not(c_odd))
+        def _():
+            for t, cc in enumerate(fast_cols(even)):
+                act(fast_col_copy(b, t, cc, even_slot, r, even_row, False))
+
+        @pl.when(c_odd)
+        def _():
+            for t, cc in enumerate(fast_cols(even)):
+                act(fast_col_copy(b, t, cc, even_slot, r, even_row, True))
+            for t in range(1, n_col):
+                act(col_copy(b, lax.rem(c + n_col - t, n_col), slot_a, r, target))
+
+            @pl.when(target != r)
+            def _():
+                act(col_copy(b, c, slot_a, r, target))
+
+            if own:
+                @pl.when(target == r)
+                def _():
+                    bpart[slot_a, r] = bacc[b]
 
     def send_col(b):
-        each_col_copy(b, lambda copy: copy.start(), True)
+        each_col_copy(b, start, True)
 
     lanes = lax.broadcasted_iota(jnp.int32, (rhs_count, rank_max), 1)
 
@@ -218,11 +392,10 @@
         return jnp.concatenate([kept, kept], axis=1)
 
     for a in range(t_rows):
-        @pl.when(r + n_row * a <= c)
+        @pl.when(below(r + n_row * a) <= c)
         def _():
             send_row(a)
 
-    v_load.wait()
     for copy in col_loads:
         copy.wait()
 
@@ -232,33 +405,72 @@
 
         @pl.when(need(r, k))
         def _():
-            for cc in range(n_col):
-                @pl.when(jnp.logical_not((r == k_row) & (c == cc)))
-                def _():
-                    row_copy(0, lax.rem(r + 1, n_row), b, cc, c).wait_recv()
-
-            x = fpart[b, 0]
-            for cc in range(1, n_col):
-                x = x + fpart[b, cc]
-            xs[b] = x
+            fast = is_fast_row(r, k)
+
+            @pl.when(jnp.logical_not(c_odd))
+            def _():
+                for cc in range(n_col):
+                    @pl.when(jnp.logical_not((r == k_row) & (c == cc)))
+                    def _():
+                        row_copy(0, lax.rem(r + 1, n_row), b, cc, c).wait_recv()
+
+                x = fpart[b, 0]
+                for cc in range(1, n_col):
+                    x = x + fpart[b, cc]
+                xs[b] = x
+
+            @pl.when(c_odd & jnp.logical_not(fast))
+            def _():
+                x_copy(b, lax.rem(r + 1, n_row)).wait_recv()
+
+            @pl.when(c_odd & fast)
+            def _():
+                away = (lax.rem(r + 1, n_row), c)
+                pair_copy(out_v.at[0], in_v.at[b], tsend.at[0, 0, 0], trecv.at[b, 0], away).wait_recv()
+                pair_copy(out_w.at[0], in_w.at[b], tsend.at[0, 0, 1], trecv.at[b, 1], away).wait_recv()
+                pair_v[...] = in_v[b].astype(BF16)
+                full = in_w[b]
+                high = full.astype(BF16)
+                pair_w[:rank_max] = high
+                pair_w[rank_max:] = (full - high.astype(F32)).astype(BF16)
+                for cc in range(n_col):
+                    fast_row_copy(0, 0, lax.rem(r + 1, n_row), b, cc, c, False).wait_recv()
+                x = epart[b, 0]
+                for cc in range(1, n_col):
+                    x = x + epart[b, cc]
+                p = dot(x.astype(BF16), pair_v[...]).astype(BF16)
+                part = dot(jnp.concatenate([p, p], axis=1), pair_w[...])
+                for cc in range(n_col):
+                    @pl.when(jnp.logical_not((r == k_row) & (c == cc)))
+                    def _():
+                        row_copy(0, lax.rem(r + 1, n_row), b, cc, c).wait_recv()
+
+                x = fpart[b, 0]
+                for cc in range(1, n_col):
+                    x = x + fpart[b, cc]
+                xs[b] = x - part
+
+            x = xs[b]
             xb = x.astype(BF16)
             for a in range(t_rows):
                 i = r + n_row * a
 
-                @pl.when(i > k)
+                @pl.when(below(i) > k)
                 def _():
                     p = live(dot(xb, v[a, b]), a, b)
                     acc[a] = acc[a] - dot(p, w[a, b])
 
-                    @pl.when(i <= k + n_col)
+                    @pl.when(below(i) <= k + n_col)
                     def _():
                         send_row(a)
 
+            each_x_copy(b, start)
+
             @pl.when(r == k_row)
             def _():
                 bacc[b] = wide_dot(xs[b], drow[k // n_row], NT)
 
-                @pl.when(k >= i_max)
+                @pl.when(above(k) >= i_max)
                 def _():
                     send_col(b)
 
@@ -274,6 +486,17 @@
                 return inner
 
             lax.fori_loop(0, t_rows * t_cols, fold_right, 0)
+            for a in range(1, t_rows):
+                send_forward_pair(a)
+            if t_cols == 1:
+                for a in reversed(range(t_rows)):
+                    send_backward_pair(a)
+
+        if t_cols > 1:
+            @pl.when(b == 1)
+            def _():
+                for a in reversed(range(t_rows)):
+                    send_backward_pair(a)
 
         return carry
 
@@ -285,42 +508,105 @@
             src_ref=part, dst_ref=part, send_sem=zsend.at[a, rr], recv_sem=zrecv.at[i],
             device_id=(rr, c), device_id_type=MESH,
         )
+
+    def z_even_copy(a, cc, i):
+        part = z_all.at[pl.ds(i * per, per)]
+        return pltpu.make_async_remote_copy(
+            src_ref=part, dst_ref=part, send_sem=esend.at[a, cc], recv_sem=zrecv.at[i],
+            device_id=(r, cc), device_id_type=MESH,
+        )
+
+    def each_z_even(a, act):
+        i = r + n_row * a
+
+        @pl.when(jnp.logical_not(r_odd) & (c == fast_cols(i)[0]))
+        def _():
+            for t in range(1, n_col):
+                cc = lax.rem(c + t, n_col)
+
+                @pl.when(jnp.logical_not(is_fast_col(cc, i)))
+                def _():
+                    act(z_even_copy(a, cc, i))
 
     for a in reversed(range(t_rows)):
         i = r + n_row * a
         i_col = lax.rem(i, n_col)
 
         def wait_part(rr, carry):
-            @pl.when(need(rr, i) & jnp.logical_not((rr == r) & (c == i_col)))
+            @pl.when(need_back(rr, i) & jnp.logical_not((rr == r) & (c == i_col)))
             def _():
                 col_copy(0, lax.rem(c + 1, n_col), a, rr, r).wait_recv()
 
             return carry
 
-        lax.fori_loop(0, n_row, wait_part, 0)
-        z = bpart[a, 0]
-        for rr in range(1, n_row):
-            z = z + bpart[a, rr]
-        for q in range(per):
-            z_all[i * per + q] = z[:, q * BLK:(q + 1) * BLK]
+        def put(z):
+            for q in range(per):
+                z_all[i * per + q] = z[:, q * BLK:(q + 1) * BLK]
+
+        fast = is_fast_col(c, i)
+
+        @pl.when(r_odd)
+        def _():
+            lax.fori_loop(0, n_row, wait_part, 0)
+            z = bpart[a, 0]
+            for rr in range(1, n_row):
+                z = z + bpart[a, rr]
+            put(z)
+
+        @pl.when(jnp.logical_not(r_odd | fast))
+        def _():
+            z_even_copy(a, lax.rem(c + 1, n_col), i).wait_recv()
+
+        @pl.when(jnp.logical_not(r_odd) & fast)
+        def _():
+            away = (r, lax.rem(c + 1, n_col))
+            pair_copy(out_u.at[0], in_u.at[a], ssend.at[0, 0, 0], srecv.at[a, 0], away).wait_recv()
+            pair_copy(out_y.at[0], in_y.at[a], ssend.at[0, 0, 1], srecv.at[a, 1], away).wait_recv()
+            pair_u[...] = in_u[a].astype(BF16)
+            full = in_y[a]
+            high = full.astype(BF16)
+            pair_y[:, :rank_max] = high
+            pair_y[:, rank_max:] = (full - high.astype(F32)).astype(BF16)
+
+            def wait_odd(rr, carry):
+                @pl.when(need_back(rr, i + 1))
+                def _():
+                    fast_col_copy(0, 0, lax.rem(c + 1, n_col), a, rr, r, True).wait_recv()
+
+                return carry
+
+            lax.fori_loop(0, n_row, wait_odd, 0)
+            z = opart[a, 0]
+            for rr in range(1, n_row):
+                z = z + opart[a, rr]
+            p = dot(z.astype(BF16), pair_u[...], NT).astype(BF16)
+            part = dot(jnp.concatenate([p, p], axis=1), pair_y[...], NT)
+            lax.fori_loop(0, n_row, wait_part, 0)
+            z = bpart[a, 0]
+            for rr in range(1, n_row):
+                z = z + bpart[a, rr]
+            put(z - part)
+
+        z = jnp.concatenate([z_all[i * per + q] for q in range(per)], axis=1)
         zb = z.astype(BF16)
 
         def back(t, carry):
             b = t_cols - 1 - t
             j = c + n_col * b
 
-            @pl.when(j < i)
+            @pl.when(above(j) < i)
             def _():
                 q = live(dot(zb, u[a, b], NT), a, b)
                 bacc[b] = bacc[b] - dot(q, y[a, b], NT)
 
-                @pl.when(j >= i - n_row)
+                @pl.when(above(j) >= i - n_row)
                 def _():
                     send_col(b)
 
             return carry
 
         lax.fori_loop(0, t_cols, back, 0)
+        each_z_even(a, start)
 
         def z_start(o, carry):
             z_copy(a, lax.rem(r + o, n_row), i).start()
@@ -349,13 +635,22 @@
         returned = dot(taken, bt[ch], NT)
         child_out[ch] = cx_ref[ch].astype(F32) - wide_dot(returned, ci[ch])
 
+    def sent(copy):
+        copy.wait_send()
+
     def csum_done(o, carry):
         csum_copy(lax.rem(r + o, n_row), r).wait_send()
         return carry
 
     lax.fori_loop(1, n_row, csum_done, 0)
     for a in range(t_rows):
-        each_row_copy(a, lambda copy: copy.wait_send(), False)
+        each_row_copy(a, sent, False)
+        each_z_even(a, sent)
+
+        @pl.when(owns(a))
+        def _():
+            each_forward_pair(a, sent)
+            each_backward_pair(a, sent)
 
         def z_done(o, carry):
             z_copy(a, lax.rem(r + o, n_row), r + n_row * a).wait_send()
@@ -363,9 +658,11 @@
 
         lax.fori_loop(1, n_row, z_done, 0)
     for b in range(t_cols):
-        @pl.when(need(r, c + n_col * b))
-        def _():
-            each_col_copy(b, lambda copy: copy.wait_send(), False)
+        @pl.when(need_back(r, c + n_col * b))
+        def _():
+            each_col_copy(b, sent, False)
+
+        each_x_copy(b, sent)
 
 
 def per_device(
@@ -408,19 +705,44 @@
             pltpu.VMEM((n_row, t_rows) + vec, F32),
             pltpu.VMEM((t_rows,) + vec, F32),
             pltpu.VMEM((t_cols, n_col) + vec, F32),
+            pltpu.VMEM((t_cols, n_col) + vec, F32),
             pltpu.VMEM((t_cols,) + vec, F32),
             pltpu.VMEM((t_cols,) + vec, F32),
             pltpu.VMEM((t_rows, n_row) + vec, F32),
+            pltpu.VMEM((t_rows, n_row) + vec, F32),
             pltpu.VMEM((ntile * tile // BLK, rhs_count, BLK), F32),
+            pltpu.VMEM((t_rows, tile, rank_max), F32),
+            pltpu.VMEM((t_rows, rank_max, tile), F32),
+            pltpu.VMEM((t_rows, rank_max, tile), F32),
+            pltpu.VMEM((t_rows, tile, rank_max), F32),
+            pltpu.VMEM((t_cols, tile, rank_max), F32),
+            pltpu.VMEM((t_cols, rank_max, tile), F32),
+            pltpu.VMEM((t_rows, rank_max, tile), F32),
+            pltpu.VMEM((t_rows, tile, rank_max), F32),
+            pltpu.VMEM((tile, rank_max), BF16),
+            pltpu.VMEM((2 * rank_max, tile), BF16),
+            pltpu.VMEM((rank_max, tile), BF16),
+            pltpu.VMEM((tile, 2 * rank_max), BF16),
             dma((4 + 2 * t_rows + t_cols,)),
             dma((n_row,)),
             dma((n_row,)),
             dma((t_rows, n_row)),
             dma((t_cols, n_col)),
+            dma((t_rows, 2)),
+            dma((t_cols, n_col)),
             dma((t_cols, n_col)),
             dma((t_rows, n_row)),
+            dma((t_cols, 2)),
+            dma((t_rows, n_row)),
+            dma((t_cols, n_row)),
+            dma((t_cols,)),
             dma((t_rows, n_row)),
             dma((ntile,)),
+            dma((t_rows, n_col)),
+            dma((t_rows, 2, 2)),
+            dma((t_cols, 2)),
+            dma((t_rows, 2, 2)),
+            dma((t_rows, 2)),
         ],
         compiler_params=pltpu.CompilerParams(collective_id=0, has_side_effects=True),
     )(

time: 117 us -> 106 us (0.906)
  Pallas kernels: 114 us -> 103 us
    pallas_call x1, Pallas kernels: 114 us -> 103 us  [per_device(): pl.pallas_call(functools.partial(solve_kernel, n_row, n_col, t_rows, t_co...]
where the time goes in v2:
time: 106 us
  Pallas kernels  103 us (97%)
  local copies, waits for them, and re-layouts  2.62 us (2%)
    pallas_call x1, Pallas kernels, per_device(): pl.pallas_call(functools.partial(solve_kernel, n_row, n_col, t_rows, t_co...  103 us
    unnamed x2, local copies, waits for them, and re-layouts  2.62 us

profile of v2, /device:TPU:0, one launch (start us, length us, event | category | flops | bytes accessed | tf_op | source)
XLA Modules:
  0.0 105.8 jit_solution(6103117215916566113)
XLA Ops:
  0.6 102.6 %shard_map.104 = (f32[8,256]{1,0:T(8,128)}, f32[1,8,512]{2,1,0:T(8,128)}) custom-call(bf16[8,8192]{1,0:T(8,128)(2,1)} %rhs_hbm.1, bf16[16,512,512]{2,1,0:T(8,128)(2,1)} %dinv_hbm.1, bf16[2,4,128,512]{3,2,1,0:T(8,128)(2,1)} %bitcast.3, bf16[2,4,512,128]{3,2,1,0:T(8,128)(2,1)} %bitcast.4, s32[2,4]{1,0:T(2,128)} %bitcast.5, bf16[1,8,512]{2,1,0:T(8,128)(2,1)} %cx_ref.1, ...), custom_call_target="tpu_custom_call" | custom-call | tf_op jit(solution)/shard_map/pallas_call | solution.py:684
  103.2 1.3 %copy.13 = f32[8,256]{1,0:T(8,128)} copy(f32[8,256]{1,0:T(8,128)} %get-tuple-element.4) | data formatting | bytes 16384
  104.5 1.3 %copy.14 = f32[1,8,512]{2,1,0:T(8,128)} copy(f32[1,8,512]{2,1,0:T(8,128)} %get-tuple-element.5) | data formatting | bytes 32768

commit v3 on v2

--- a/solution.py
+++ b/solution.py
@@ -106,11 +106,10 @@
         return (row == first) | (both & (row == second))
 
     def fast_cols(even):
-        return lax.rem(even + n_col - 1, n_col), lax.rem(even + n_col - 2, n_col)
+        return (lax.rem(even + n_col - 1, n_col),)
 
     def is_fast_col(col, even):
-        first, second = fast_cols(even)
-        return (col == first) | (col == second)
+        return col == fast_cols(even)[0]
 
     for a in range(t_rows):
         i = r + n_row * a
@@ -160,6 +159,7 @@
     for copy in row_loads:
         copy.wait()
     u_load.wait()
+    v_load.wait()
 
     def fold_left(t, carry):
         a = t // t_cols
@@ -170,8 +170,6 @@
         w[a, b, rank_max:] = (full - high.astype(F32)).astype(BF16)
         return carry
 
-    lax.fori_loop(0, t_rows * t_cols, fold_left, 0)
-    v_load.wait()
 
     def owns(a):
         return r_odd & (lax.rem(r + n_row * a + n_col - 1, n_col) == c)
@@ -216,7 +214,7 @@
             rank = rank_ref[a, b]
             keep = lax.broadcasted_iota(jnp.int32, (tile, rank_max), 1) < rank
             out_v[a] = jnp.where(keep, v[a, b].astype(F32), 0.0)
-            out_w[a] = w[a, b, :rank_max].astype(F32) + w[a, b, rank_max:].astype(F32)
+            out_w[a] = dot(u[a, b], drow[a])
             each_forward_pair(a, start)
 
     def send_backward_pair(a):
@@ -230,6 +228,7 @@
             each_backward_pair(a, start)
 
     send_forward_pair(0)
+    lax.fori_loop(0, t_rows * t_cols, fold_left, 0)
 
     def csum_wait(o, carry):
         rr = lax.rem(r + o, n_row)
@@ -493,9 +492,9 @@
                     send_backward_pair(a)
 
         if t_cols > 1:
-            @pl.when(b == 1)
-            def _():
-                for a in reversed(range(t_rows)):
+            for step, a in enumerate(reversed(range(t_rows))):
+                @pl.when(b == min(1 + step, t_cols - 1))
+                def _():
                     send_backward_pair(a)
 
         return carry
@@ -522,11 +521,7 @@
         @pl.when(jnp.logical_not(r_odd) & (c == fast_cols(i)[0]))
         def _():
             for t in range(1, n_col):
-                cc = lax.rem(c + t, n_col)
-
-                @pl.when(jnp.logical_not(is_fast_col(cc, i)))
-                def _():
-                    act(z_even_copy(a, cc, i))
+                act(z_even_copy(a, lax.rem(c + n_col - t, n_col), i))
 
     for a in reversed(range(t_rows)):
         i = r + n_row * a
@@ -588,6 +583,7 @@
             put(z - part)
 
         z = jnp.concatenate([z_all[i * per + q] for q in range(per)], axis=1)
+        each_z_even(a, start)
         zb = z.astype(BF16)
 
         def back(t, carry):
@@ -606,7 +602,6 @@
             return carry
 
         lax.fori_loop(0, t_cols, back, 0)
-        each_z_even(a, start)
 
         def z_start(o, carry):
             z_copy(a, lax.rem(r + o, n_row), i).start()

time: 106 us -> 101 us (0.953)
  Pallas kernels: 103 us -> 97.6 us
    pallas_call x1, Pallas kernels: 103 us -> 97.6 us  [per_device(): pl.pallas_call(functools.partial(solve_kernel, n_row, n_col, t_rows, t_co...]
where the time goes in v3:
time: 101 us
  Pallas kernels  97.6 us (97%)
  local copies, waits for them, and re-layouts  2.62 us (3%)
    pallas_call x1, Pallas kernels, per_device(): pl.pallas_call(functools.partial(solve_kernel, n_row, n_col, t_rows, t_co...  97.6 us
    unnamed x2, local copies, waits for them, and re-layouts  2.62 us

profile of v3, /device:TPU:0, one launch (start us, length us, event | category | flops | bytes accessed | tf_op | source)
XLA Modules:
  0.0 100.9 jit_solution(9820857973405338613)
XLA Ops:
  0.6 97.6 %shard_map.104 = (f32[8,256]{1,0:T(8,128)}, f32[1,8,512]{2,1,0:T(8,128)}) custom-call(bf16[8,8192]{1,0:T(8,128)(2,1)} %rhs_hbm.1, bf16[16,512,512]{2,1,0:T(8,128)(2,1)} %dinv_hbm.1, bf16[2,4,128,512]{3,2,1,0:T(8,128)(2,1)} %bitcast.3, bf16[2,4,512,128]{3,2,1,0:T(8,128)(2,1)} %bitcast.4, s32[2,4]{1,0:T(2,128)} %bitcast.5, bf16[1,8,512]{2,1,0:T(8,128)(2,1)} %cx_ref.1, ...), custom_call_target="tpu_custom_call" | custom-call | tf_op jit(solution)/shard_map/pallas_call | solution.py:679
  98.2 1.3 %copy.13 = f32[8,256]{1,0:T(8,128)} copy(f32[8,256]{1,0:T(8,128)} %get-tuple-element.4) | data formatting | bytes 16384
  99.5 1.3 %copy.14 = f32[1,8,512]{2,1,0:T(8,128)} copy(f32[1,8,512]{2,1,0:T(8,128)} %get-tuple-element.5) | data formatting | bytes 32768
